TPU v7x, 128 devices: a whole 4x4x4 slice. The times are simulated.
128 devices in a mesh: dp: 16 (over y, z_lo, core), ep: 8 (over z_hi, x).
Axes of the slice: x: 4, y: 4, z: 4 (z_hi: 2, z_lo: 2; z = z_hi * 2 + z_lo), core: 2. Of those that a mesh axis runs over, the one named last changes fastest.
Arguments:
- tokens: bfloat16 [16384, 6144], P(('dp', 'ep')), may hold values from -6 to 6
- out_grad: bfloat16 [16384, 6144], P(('dp', 'ep')), may hold values from -0.75 to 0.75
- expert_ids: int32 [16384, 2], P(('dp', 'ep')), may hold values from 0 to 7, all different within a row; in each aligned block of 128 rows (0 to 127, 128 to 255, ...) at most 40 rows name the same one
- route_weight: float32 [16384, 2], P(('dp', 'ep')), may hold values from 0.2 to 1
- w_gate: bfloat16 [8, 6144, 256], P('ep', 'dp'), may hold values from -0.078125 to 0.078125
- w_up: bfloat16 [8, 6144, 256], P('ep', 'dp'), may hold values from -0.078125 to 0.078125
- w_down: bfloat16 [8, 256, 6144], P('ep', None, 'dp'), may hold values from -0.375 to 0.375
Outputs:
- d_tokens: bfloat16 [16384, 6144], P(('dp', 'ep'))
- grad_gate: float32 [8, 6144, 256], P('ep', 'dp')
- grad_up: float32 [8, 6144, 256], P('ep', 'dp')
- grad_down: float32 [8, 256, 6144], P('ep', None, 'dp')
Inputs may be any that keep to these rules, and one draw needn't show every extreme that they name: `expert_ids`: each token names two different experts. Among the 128 tokens of one device (aligned blocks of 128 rows) no expert is named more than 40 times, and in some blocks one expert is named exactly 40 times.
All inputs are finite; a program needn't handle non-finite values.
Results may differ from a plain program's by a relative error of at most 0.0065.
Values may be sent and summed in bfloat16 or wider, within the bound.
A program may use at most 128 MiB of HBM per device.

v0:
```python
import jax
import jax.numpy as jnp
from jax import lax
from jax.sharding import PartitionSpec as P


def in_one_piece(arrays, axis, dim, along):
    widths = [a.shape[along] for a in arrays]
    both = jnp.concatenate(arrays, axis=along)
    result = lax.all_gather(both, axis, axis=dim, tiled=True)
    return tuple(jnp.split(result, [sum(widths[:k]) for k in range(1, len(widths))], axis=along))


def contract_rows(left, right):
    return lax.dot_general(
        left, right, (((0,), (0,)), ((), ())), preferred_element_type=jnp.float32
    )


def contract_last(left, right):
    return lax.dot_general(
        left, right, (((1,), (1,)), ((), ())), preferred_element_type=jnp.float32
    )


def shards(tokens, out_grad, expert_ids, route_weight, w_gate, w_up, w_down):
    tok_dev, width = tokens.shape
    experts = lax.axis_size("ep")
    capacity = 10 * tok_dev // (4 * experts)
    flat_ids = expert_ids.reshape(-1)
    onehot = (flat_ids[:, None] == jnp.arange(experts, dtype=jnp.int32)).astype(jnp.int32)
    slot_rank = jnp.sum((jnp.cumsum(onehot, axis=0) - onehot) * onehot, axis=1)
    slot_index = flat_ids * capacity + slot_rank
    pair_rows = jnp.repeat(tokens, 2, axis=0)
    scaled = (
        route_weight.reshape(-1)[:, None] * jnp.repeat(out_grad, 2, axis=0).astype(jnp.float32)
    ).astype(jnp.bfloat16)
    empty = jnp.zeros((experts * capacity, width), jnp.bfloat16)
    send_rows = empty.at[slot_index].set(pair_rows).reshape(experts, capacity, width)
    send_scaled = empty.at[slot_index].set(scaled).reshape(experts, capacity, width)
    recv_rows, recv_scaled = (
        lax.all_to_all(send_rows, "ep", split_axis=0, concat_axis=0, tiled=True),
        lax.all_to_all(send_scaled, "ep", split_axis=0, concat_axis=0, tiled=True),
    )
    x_rows = recv_rows.reshape(-1, width)
    grad_out = recv_scaled.reshape(-1, width)
    gate_w, up_w = in_one_piece((w_gate[0], w_up[0]), "dp", 0, 1)
    gate_pre = jnp.dot(x_rows, gate_w, preferred_element_type=jnp.float32)
    up_pre = jnp.dot(x_rows, up_w, preferred_element_type=jnp.float32)
    grad_hidden = contract_last(grad_out, lax.all_gather(w_down[0], "dp", axis=1, tiled=True))
    sigmoid_a = jax.nn.sigmoid(gate_pre)
    silu_a = gate_pre * sigmoid_a
    hidden = (silu_a * up_pre).astype(jnp.bfloat16)
    grad_gate_pre = (
        grad_hidden * up_pre * sigmoid_a * (1.0 + gate_pre * (1.0 - sigmoid_a))
    ).astype(jnp.bfloat16)
    grad_up_pre = (grad_hidden * silu_a).astype(jnp.bfloat16)
    pair_grad = (contract_last(grad_gate_pre, gate_w) + contract_last(grad_up_pre, up_w)).astype(
        jnp.bfloat16
    )
    back = lax.all_to_all(
        pair_grad.reshape(experts, capacity, width), "ep", split_axis=0, concat_axis=0, tiled=True
    )
    picked = back.reshape(-1, width)[slot_index].reshape(tok_dev, 2, width)
    d_tokens = jnp.sum(picked.astype(jnp.float32), axis=1).astype(jnp.bfloat16)
    column_rows, column_grad = (
        lax.all_to_all(x_rows, "dp", split_axis=1, concat_axis=0, tiled=True),
        lax.all_to_all(grad_out, "dp", split_axis=1, concat_axis=0, tiled=True),
    )
    every_gate, every_up, every_hidden = in_one_piece(
        (grad_gate_pre, grad_up_pre, hidden), "dp", 0, 1
    )
    shard_gate = contract_rows(column_rows, every_gate)
    shard_up = contract_rows(column_rows, every_up)
    shard_down = contract_rows(column_grad, every_hidden)
    return (d_tokens, shard_gate[None], shard_up[None], jnp.transpose(shard_down)[None])


def solution(mesh):
    in_specs = (
        P(("dp", "ep"), None),
        P(("dp", "ep"), None),
        P(("dp", "ep"), None),
        P(("dp", "ep"), None),
        P("ep", "dp", None),
        P("ep", "dp", None),
        P("ep", None, "dp"),
    )
    out_specs = (
        P(("dp", "ep"), None),
        P("ep", "dp", None),
        P("ep", "dp", None),
        P("ep", None, "dp"),
    )
    return jax.shard_map(shards, mesh=mesh, in_specs=in_specs, out_specs=out_specs, check_vma=False)
```

profile of v0, /device:TPU:55, one launch (start us, length us, event | category | flops | bytes accessed | tf_op | source)
XLA Modules:
  0.0 404.8 jit_solution(12341281554003499555)
XLA Ops:
  7.2 0.0 all-gather.9.cloned.1.call-start
  7.2 0.7 all-gather.9.cloned.1.call-update
  7.9 0.0 all-gather.5.cloned.1.call-start
  7.9 1.8 pad_maximum_fusion.1
  9.7 0.0 all-gather.5.cloned.1.call-update
  9.8 0.8 copy.22
  10.6 0.1 eq.29
  10.7 0.1 eq.25
  10.8 0.6 reduce-window.6
  11.4 0.2 slice_reduce_fusion
  11.7 0.7 broadcast_multiply_fusion
  12.4 0.1 copy.21
  12.5 0.1 mul.52
  12.6 6.8 %broadcast_in_dim.23 = f32[128,2,6144]{2,1,0:T(2,128)} broadcast(bf16[128,6144]{1,0:T(8,128)(2,1)} %param.8), dimensions={0,2} | broadcast | bytes 7864320 | tf_op jit(solution)/shard_map/broadcast_in_dim | solution.py:36
  19.5 0.0 copy-start.1
  19.5 8.4 %convert_element_type.34 = f32[256,6144]{1,0:T(8,128)} reshape(f32[128,2,6144]{2,1,0:T(2,128)} %broadcast_in_dim.23) | data formatting | bytes 12582912 | tf_op jit(solution)/shard_map/convert_element_type | solution.py:36
  27.9 0.0 copy-done.1
  27.9 0.1 copy.24
  28.0 0.1 mul.54
  28.1 0.1 fusion.32
  28.2 9.5 %scatter_custom_fusion = bf16[320,6144]{1,0:T(8,128)(2,1)} fusion(s32[256]{0:T(256)S(1)} %bitcast.56, f32[256,6144]{1,0:T(8,128)} %convert_element_type.34, f32[256]{0:T(256)S(1)} %mul.54, bf16[]{:T(256)} %constant.5.clone.1), kind=kCustom, calls=%fused_computation.6 | custom fusion | flops 3145728 | bytes 10224642 | tf_op jit(solution)/shard_map/scatter | solution.py:40
  37.7 7.3 %all-to-all-start = ((bf16[8,40,6144]{2,1,0:T(8,128)(2,1)}), bf16[8,40,6144]{2,1,0:T(8,128)(2,1)}, u32[]{:S(2)}, u32[]{:S(2)}) async-start(bf16[8,40,6144]{2,1,0:T(8,128)(2,1)} %bitcast.49), calls=%async_computation | async-start | bytes 7864320 | tf_op jit(solution)/shard_map/all_to_all | solution.py:43
  45.0 3.3 broadcast_in_dim.24
  48.3 2.7 reshape.118
  51.0 8.4 %scatter_custom_fusion.1 = bf16[320,6144]{1,0:T(8,128)(2,1)} fusion(s32[256]{0:T(256)S(1)} %bitcast.57, bf16[256,6144]{1,0:T(8,128)(2,1)} %reshape.118, bf16[]{:T(256)} %constant.5.clone.1), kind=kCustom, calls=%fused_computation.23 | custom fusion | bytes 3932672 | tf_op jit(solution)/shard_map/scatter | solution.py:39
  59.5 42.4 %all-to-all-done = bf16[8,40,6144]{2,1,0:T(8,128)(2,1)} async-done(((bf16[8,40,6144]{2,1,0:T(8,128)(2,1)}), bf16[8,40,6144]{2,1,0:T(8,128)(2,1)}, u32[]{:S(2)}, u32[]{:S(2)}) %all-to-all-start) | async-done | bytes 3932192 | tf_op jit(solution)/shard_map/all_to_all | solution.py:43
  101.9 6.4 %all-to-all-start.1 = ((bf16[8,40,6144]{2,1,0:T(8,128)(2,1)}), bf16[8,40,6144]{2,1,0:T(8,128)(2,1)}, u32[]{:S(2)}, u32[]{:S(2)}) async-start(bf16[8,40,6144]{2,1,0:T(8,128)(2,1)} %bitcast.48), calls=%async_computation.1 | async-start | bytes 7864320 | tf_op jit(solution)/shard_map/all_to_all | solution.py:42
  108.3 0.2 all-gather.7.cloned.1.call-start
  108.4 0.0 all-gather.9.cloned.1.call-done
  108.5 4.4 %fusion.2 = f32[320,256]{1,0:T(8,128)S(1)} fusion(bf16[320,6144]{1,0:T(8,128)(2,1)} %bitcast.5, bf16[1,256,6144]{2,1,0:T(8,128)(2,1)} %all-gather.9.cloned.1.call-done), kind=kOutput, calls=%fused_computation.7 | convolution fusion | flops 1006632960 | bytes 7405568 | tf_op jit(solution)/shard_map/dot_general | solution.py:21
  112.9 47.6 %all-to-all-done.1 = bf16[8,40,6144]{2,1,0:T(8,128)(2,1)} async-done(((bf16[8,40,6144]{2,1,0:T(8,128)(2,1)}), bf16[8,40,6144]{2,1,0:T(8,128)(2,1)}, u32[]{:S(2)}, u32[]{:S(2)}) %all-to-all-start.1) | async-done | bytes 3932192 | tf_op jit(solution)/shard_map/all_to_all | solution.py:42
  160.5 0.0 all-gather.5.cloned.1.call-done
  160.5 0.0 copy-start
  160.5 4.4 %fusion.7 = f32[320,256]{1,0:T(8,128)S(1)} fusion(bf16[320,6144]{1,0:T(8,128)(2,1)} %bitcast.8, bf16[6144,512]{1,0:T(8,128)(2,1)} %all-gather.5.cloned.1.call-done), kind=kOutput, calls=%fused_computation.12 | convolution fusion | flops 1006632960 | bytes 7405568 | tf_op jit(solution)/shard_map/dot_general | solution.py:48
  164.9 0.5 copy-done
  165.4 3.3 multiply_convert_fusion.2
  168.7 0.8 pad_maximum_fusion
  169.5 0.0 all-gather.7.cloned.1.call-update
  169.6 3.0 copy.27
  172.5 2.8 copy.25
  175.4 0.0 slice-start
  175.4 8.4 %all-to-all-start.3 = ((bf16[320,16,384]{2,0,1:T(8,128)(2,1)}), bf16[320,16,384]{2,0,1:T(8,128)(2,1)}, u32[]{:S(2)}, u32[]{:S(2)}) async-start(bf16[320,16,384]{2,0,1:T(8,128)(2,1)} %copy.25), calls=%async_computation.3 | async-start | bytes 7864320 | tf_op jit(solution)/shard_map/all_to_all | solution.py:67
  183.8 0.0 slice-start.1
  183.8 3.3 fusion.5
  187.0 0.0 slice-done
  187.1 0.0 slice-done.1
  187.1 3.2 fusion
  190.3 68.9 %all-to-all-done.3 = bf16[320,16,384]{2,0,1:T(8,128)(2,1)} async-done(((bf16[320,16,384]{2,0,1:T(8,128)(2,1)}), bf16[320,16,384]{2,0,1:T(8,128)(2,1)}, u32[]{:S(2)}, u32[]{:S(2)}) %all-to-all-start.3) | async-done | bytes 3932192 | tf_op jit(solution)/shard_map/all_to_all | solution.py:67
  259.2 6.4 %all-to-all-start.2 = ((bf16[8,40,6144]{2,1,0:T(8,128)(2,1)}), bf16[8,40,6144]{2,1,0:T(8,128)(2,1)}, u32[]{:S(2)}, u32[]{:S(2)}) async-start(bf16[8,40,6144]{2,1,0:T(8,128)(2,1)} %bitcast.47), calls=%async_computation.2 | async-start | bytes 7864320 | tf_op jit(solution)/shard_map/all_to_all | solution.py:61
  265.6 3.0 copy.28
  268.6 2.8 copy.26
  271.4 51.4 %all-to-all-done.2 = bf16[8,40,6144]{2,1,0:T(8,128)(2,1)} async-done(((bf16[8,40,6144]{2,1,0:T(8,128)(2,1)}), bf16[8,40,6144]{2,1,0:T(8,128)(2,1)}, u32[]{:S(2)}, u32[]{:S(2)}) %all-to-all-start.2) | async-done | bytes 3932192 | tf_op jit(solution)/shard_map/all_to_all | solution.py:61
  322.8 14.8 %all-to-all-start.4 = ((bf16[320,16,384]{2,0,1:T(8,128)(2,1)}), bf16[320,16,384]{2,0,1:T(8,128)(2,1)}, u32[]{:S(2)}, u32[]{:S(2)}) async-start(bf16[320,16,384]{2,0,1:T(8,128)(2,1)} %copy.26), calls=%async_computation.4 | async-start | bytes 7864320 | tf_op jit(solution)/shard_map/all_to_all | solution.py:68
  337.6 9.7 %gather_fusion = bf16[256,6144]{1,0:T(8,128)(2,1)} fusion(bf16[320,6144]{1,0:T(8,128)(2,1)} %bitcast.12, s32[1024]{0:T(1024)S(1)} %pad_clamp_fusion), kind=kCustom, calls=%fused_computation | custom fusion | bytes 6292480 | tf_op jit(solution)/shard_map/gather | solution.py:64
  347.3 6.2 %reshape.97 = bf16[128,2,6144]{2,1,0:T(2,128)(2,1)S(1)} reshape(bf16[256,6144]{1,0:T(8,128)(2,1)} %gather_fusion) | data formatting | bytes 6291456 | tf_op jit(solution)/shard_map/reshape | solution.py:64
  353.5 9.7 %reduce_sum.25 = bf16[128,6144]{1,0:T(8,128)(2,1)} reduce(bf16[128,2,6144]{2,1,0:T(2,128)(2,1)S(1)} %reshape.97, bf16[]{:T(256)} %constant.5.clone.1), dimensions={1}, to_apply=%region_5.6 | reduce | flops 786432 | bytes 4718594 | tf_op jit(solution)/shard_map/reduce_sum | solution.py:65
  363.3 0.0 all-gather.7.cloned.1.call-done
  363.3 4.9 %fusion.24 = f32[1,384,256]{2,1,0:T(8,128)} fusion(bf16[5120,384]{1,0:T(8,128)(2,1)} %bitcast.14, bf16[5120,768]{1,0:T(8,128)(2,1)} %all-gather.7.cloned.1.call-done), kind=kOutput, calls=%fused_computation.27 | convolution fusion | flops 1006632960 | bytes 6946816 | tf_op jit(solution)/shard_map/dot_general | solution.py:15
  368.2 4.9 %fusion.21 = f32[1,384,256]{2,1,0:T(8,128)} fusion(bf16[5120,384]{1,0:T(8,128)(2,1)} %bitcast.14, bf16[5120,768]{1,0:T(8,128)(2,1)} %all-gather.7.cloned.1.call-done), kind=kOutput, calls=%fused_computation.26 | convolution fusion | flops 1006632960 | bytes 6946816 | tf_op jit(solution)/shard_map/dot_general | solution.py:15
  373.1 19.6 %all-to-all-done.4 = bf16[320,16,384]{2,0,1:T(8,128)(2,1)} async-done(((bf16[320,16,384]{2,0,1:T(8,128)(2,1)}), bf16[320,16,384]{2,0,1:T(8,128)(2,1)}, u32[]{:S(2)}, u32[]{:S(2)}) %all-to-all-start.4) | async-done | bytes 3932192 | tf_op jit(solution)/shard_map/all_to_all | solution.py:68
  392.6 5.2 %fusion.27 = f32[1,256,384]{2,1,0:T(8,128)} fusion(bf16[5120,384]{1,0:T(8,128)(2,1)} %bitcast.19, bf16[5120,768]{1,0:T(8,128)(2,1)} %all-gather.7.cloned.1.call-done), kind=kOutput, calls=%fused_computation.28 | convolution fusion | flops 1006632960 | bytes 6946816 | tf_op jit(solution)/shard_map/dot_general | solution.py:15
  (6 shorter events, 0.1 us)
Async XLA Ops:
  7.2 101.3 %all-gather.9.cloned.1.call-start = ((), (), s32[]{:S(2)}) async-start(), calls=%async_computation.7 | async-start | bytes 3342336 | tf_op jit(solution)/shard_map/all_gather | solution.py:50
  7.9 152.6 %all-gather.5.cloned.1.call-start = ((), (), s32[]{:S(2)}) async-start(), calls=%async_computation.5 | async-start | bytes 6684672 | tf_op jit(solution)/shard_map/all_gather | solution.py:10
  19.5 8.4 %copy-start.1 = (f32[128,2]{0,1:T(2,128)S(1)}, f32[128,2]{0,1:T(2,128)}, u32[]{:S(2)}) copy-start(f32[128,2]{0,1:T(2,128)} %param.10) | copy-start | bytes 3076
  37.7 64.2 %all-to-all-start = ((bf16[8,40,6144]{2,1,0:T(8,128)(2,1)}), bf16[8,40,6144]{2,1,0:T(8,128)(2,1)}, u32[]{:S(2)}, u32[]{:S(2)}) async-start(bf16[8,40,6144]{2,1,0:T(8,128)(2,1)} %bitcast.49), calls=%async_computation | async-start | bytes 7864320 | tf_op jit(solution)/shard_map/all_to_all | solution.py:43
  101.9 58.6 %all-to-all-start.1 = ((bf16[8,40,6144]{2,1,0:T(8,128)(2,1)}), bf16[8,40,6144]{2,1,0:T(8,128)(2,1)}, u32[]{:S(2)}, u32[]{:S(2)}) async-start(bf16[8,40,6144]{2,1,0:T(8,128)(2,1)} %bitcast.48), calls=%async_computation.1 | async-start | bytes 7864320 | tf_op jit(solution)/shard_map/all_to_all | solution.py:42
  108.3 255.0 %all-gather.7.cloned.1.call-start = ((), (), s32[]{:S(2)}) async-start(), calls=%async_computation.6 | async-start | bytes 8355840 | tf_op jit(solution)/shard_map/all_gather | solution.py:10
  160.5 4.9 %copy-start = (bf16[6144,512]{1,0:T(8,128)(2,1)S(1)}, bf16[6144,512]{1,0:T(8,128)(2,1)}, u32[]{:S(2)}) copy-start(bf16[6144,512]{1,0:T(8,128)(2,1)} %all-gather.5.cloned.1.call-done) | copy-start | bytes 18874372
  175.4 11.7 %slice-start = ((s8[6291456]{0:T(1024)(128)(4,1)}), s8[2097152]{0:T(1024)(128)(4,1)S(1)}, s32[]{:S(2)}) async-start(s8[6291456]{0:T(1024)(128)(4,1)} %bitcast.52), calls=%async_computation.8 | async-start | bytes 4194304
  175.4 83.8 %all-to-all-start.3 = ((bf16[320,16,384]{2,0,1:T(8,128)(2,1)}), bf16[320,16,384]{2,0,1:T(8,128)(2,1)}, u32[]{:S(2)}, u32[]{:S(2)}) async-start(bf16[320,16,384]{2,0,1:T(8,128)(2,1)} %copy.25), calls=%async_computation.3 | async-start | bytes 7864320 | tf_op jit(solution)/shard_map/all_to_all | solution.py:67
  183.8 3.3 slice-start.1
  259.2 63.6 %all-to-all-start.2 = ((bf16[8,40,6144]{2,1,0:T(8,128)(2,1)}), bf16[8,40,6144]{2,1,0:T(8,128)(2,1)}, u32[]{:S(2)}, u32[]{:S(2)}) async-start(bf16[8,40,6144]{2,1,0:T(8,128)(2,1)} %bitcast.47), calls=%async_computation.2 | async-start | bytes 7864320 | tf_op jit(solution)/shard_map/all_to_all | solution.py:61
  322.8 69.8 %all-to-all-start.4 = ((bf16[320,16,384]{2,0,1:T(8,128)(2,1)}), bf16[320,16,384]{2,0,1:T(8,128)(2,1)}, u32[]{:S(2)}, u32[]{:S(2)}) async-start(bf16[320,16,384]{2,0,1:T(8,128)(2,1)} %copy.26), calls=%async_computation.4 | async-start | bytes 7864320 | tf_op jit(solution)/shard_map/all_to_all | solution.py:68
Sparse Core Ops, SparseCore 0:
  9.6 36.6 all-gather.8
  48.7 85.5 all-gather.4
  169.7 97.7 all-gather.6
where the time goes:
time: 412 us; the launch traced here: 405 us
  waiting for transfers between devices  231 us (56%)
  local copies, waits for them, and re-layouts  59.4 us (14%)
  starting transfers between devices  43.5 us (11%)
  matrix products  33.6 us (8%)
  other arithmetic  23.3 us (6%)
  between operations  14.3 us (3%)
    all_to_all x1, waiting for transfers between devices, shards(): lax.all_to_all(x_rows, 'dp', split_axis=1, concat_axis=0, tiled=True)  68.9 us
    all_to_all x1, waiting for transfers between devices, shards(): lax.all_to_all(pair_grad.reshape(experts, capacity, width), 'ep', split_a...  51.4 us
    all_to_all x1, waiting for transfers between devices, shards(): lax.all_to_all(send_rows, 'ep', split_axis=0, concat_axis=0, tiled=True)  47.6 us
    all_to_all x1, waiting for transfers between devices, shards(): lax.all_to_all(send_scaled, 'ep', split_axis=0, concat_axis=0, tiled=True)  42.4 us
    all_to_all x1, waiting for transfers between devices, shards(): lax.all_to_all(grad_out, 'dp', split_axis=1, concat_axis=0, tiled=True)  19.6 us
    dot_general x3, matrix products, contract_rows(): lax.dot_general(left, right, (((0,), (0,)), ((), ())), preferred_element_...  15 us
    all_to_all x1, starting transfers between devices, shards(): lax.all_to_all(grad_out, 'dp', split_axis=1, concat_axis=0, tiled=True)  14.8 us
    dot_general x3, matrix products, contract_last(): lax.dot_general(left, right, (((1,), (1,)), ((), ())), preferred_element_...  10.9 us
  transfers between devices with their start and end apart: 8, of which 5 were waited for; matrix products, arithmetic and copies ran while one was open for 25% of the time, Pallas kernels for 0%

commit v1 on v0

--- a/solution.py
+++ b/solution.py
@@ -64,7 +64,10 @@
     picked = back.reshape(-1, width)[slot_index].reshape(tok_dev, 2, width)
     d_tokens = jnp.sum(picked.astype(jnp.float32), axis=1).astype(jnp.bfloat16)
     column_rows, column_grad = (
-        lax.all_to_all(x_rows, "dp", split_axis=1, concat_axis=0, tiled=True),
+        jnp.concatenate(
+            lax.all_to_all(jnp.stack(jnp.split(x_rows, lax.axis_size("dp"), axis=1)), "dp", 0, 0),
+            axis=0,
+        ),
         lax.all_to_all(grad_out, "dp", split_axis=1, concat_axis=0, tiled=True),
     )
     every_gate, every_up, every_hidden = in_one_piece(

time: 412 us -> 419 us (1.017)
  local copies, waits for them, and re-layouts: 59.4 us -> 80.5 us
  starting transfers between devices: 43.5 us -> 34.8 us
  waiting for transfers between devices: 231 us -> 225 us
    unnamed x12 -> x26, local copies, waits for them, and re-layouts: 7.33 us -> 29.5 us
    all_to_all x1, starting transfers between devices: 14.8 us -> 7.32 us  [shards(): lax.all_to_all(grad_out, 'dp', split_axis=1, concat_axis=0, tiled=True)]
    all_to_all x1, waiting for transfers between devices: 68.9 us -> 63 us  [shards(): lax.all_to_all(jnp.stack(jnp.split(x_rows, lax.axis_size('dp'), axis=1)),...]
  transfers between devices with their start and end apart: 8 -> 8, of which waited for: 5 -> 5; matrix products, arithmetic and copies ran while one was open for 25% -> 30% of each run, Pallas kernels for 0% -> 0%
where the time goes in v1:
time: 419 us; the launch traced here: 411 us
  waiting for transfers between devices  225 us (54%)
  local copies, waits for them, and re-layouts  80.5 us (19%)
  starting transfers between devices  34.8 us (8%)
  matrix products  33.7 us (8%)
  other arithmetic  23.3 us (6%)
  between operations  14.3 us (3%)
    all_to_all x1, waiting for transfers between devices, shards(): lax.all_to_all(jnp.stack(jnp.split(x_rows, lax.axis_size('dp'), axis=1)),...  63 us
    all_to_all x1, waiting for transfers between devices, shards(): lax.all_to_all(pair_grad.reshape(experts, capacity, width), 'ep', split_a...  51.3 us
    all_to_all x1, waiting for transfers between devices, shards(): lax.all_to_all(send_rows, 'ep', split_axis=0, concat_axis=0, tiled=True)  47.6 us
    all_to_all x1, waiting for transfers between devices, shards(): lax.all_to_all(send_scaled, 'ep', split_axis=0, concat_axis=0, tiled=True)  42.4 us
    unnamed x26, local copies, waits for them, and re-layouts  29.5 us
    all_to_all x1, waiting for transfers between devices, shards(): lax.all_to_all(grad_out, 'dp', split_axis=1, concat_axis=0, tiled=True)  19.6 us
    dot_general x3, matrix products, contract_rows(): lax.dot_general(left, right, (((0,), (0,)), ((), ())), preferred_element_...  15 us
    dot_general x3, matrix products, contract_last(): lax.dot_general(left, right, (((1,), (1,)), ((), ())), preferred_element_...  11 us
  transfers between devices with their start and end apart: 8, of which 5 were waited for; matrix products, arithmetic and copies ran while one was open for 30% of the time, Pallas kernels for 0%

profile of v1, /device:TPU:55, one launch (start us, length us, event | category | flops | bytes accessed | tf_op | source)
XLA Modules:
  0.0 411.3 jit_solution(16494814187247713524)
XLA Ops:
  7.2 0.0 all-gather.9.cloned.1.call-start
  7.2 0.7 all-gather.9.cloned.1.call-update
  7.9 0.0 all-gather.5.cloned.1.call-start
  7.9 1.8 pad_maximum_fusion.1
  9.8 0.8 copy.21
  10.6 0.1 eq.29
  10.7 0.1 eq.25
  10.8 0.7 broadcast_multiply_fusion
  11.5 0.1 copy.20
  11.6 0.1 mul.52
  11.8 0.6 reduce-window.6
  12.4 0.2 slice_reduce_fusion
  12.6 6.8 %broadcast_in_dim.23 = f32[128,2,6144]{2,1,0:T(2,128)} broadcast(bf16[128,6144]{1,0:T(8,128)(2,1)} %param.8), dimensions={0,2} | broadcast | bytes 7864320 | tf_op jit(solution)/shard_map/broadcast_in_dim | solution.py:36
  19.5 8.4 %convert_element_type.34 = f32[256,6144]{1,0:T(8,128)} reshape(f32[128,2,6144]{2,1,0:T(2,128)} %broadcast_in_dim.23) | data formatting | bytes 12582912 | tf_op jit(solution)/shard_map/convert_element_type | solution.py:36
  27.9 0.1 copy.23
  28.0 0.1 mul.54
  28.1 0.1 fusion.48
  28.2 9.5 %scatter_custom_fusion = bf16[320,6144]{1,0:T(8,128)(2,1)} fusion(s32[256]{0:T(256)S(1)} %bitcast.114, f32[256,6144]{1,0:T(8,128)} %convert_element_type.34, f32[256]{0:T(256)S(1)} %mul.54, bf16[]{:T(256)} %constant.5.clone.1), kind=kCustom, calls=%fused_computation.6 | custom fusion | flops 3145728 | bytes 10224642 | tf_op jit(solution)/shard_map/scatter | solution.py:40
  37.7 7.3 %all-to-all-start = ((bf16[8,40,6144]{2,1,0:T(8,128)(2,1)}), bf16[8,40,6144]{2,1,0:T(8,128)(2,1)}, u32[]{:S(2)}, u32[]{:S(2)}) async-start(bf16[8,40,6144]{2,1,0:T(8,128)(2,1)} %bitcast.108), calls=%async_computation | async-start | bytes 7864320 | tf_op jit(solution)/shard_map/all_to_all | solution.py:43
  45.0 3.3 broadcast_in_dim.24
  48.3 2.7 reshape.118
  51.0 8.4 %scatter_custom_fusion.1 = bf16[320,6144]{1,0:T(8,128)(2,1)} fusion(s32[256]{0:T(256)S(1)} %bitcast.115, bf16[256,6144]{1,0:T(8,128)(2,1)} %reshape.118, bf16[]{:T(256)} %constant.5.clone.1), kind=kCustom, calls=%fused_computation.23 | custom fusion | bytes 3932672 | tf_op jit(solution)/shard_map/scatter | solution.py:39
  59.5 42.4 %all-to-all-done = bf16[8,40,6144]{2,1,0:T(8,128)(2,1)} async-done(((bf16[8,40,6144]{2,1,0:T(8,128)(2,1)}), bf16[8,40,6144]{2,1,0:T(8,128)(2,1)}, u32[]{:S(2)}, u32[]{:S(2)}) %all-to-all-start) | async-done | bytes 3932192 | tf_op jit(solution)/shard_map/all_to_all | solution.py:43
  101.9 6.4 %all-to-all-start.1 = ((bf16[8,40,6144]{2,1,0:T(8,128)(2,1)}), bf16[8,40,6144]{2,1,0:T(8,128)(2,1)}, u32[]{:S(2)}, u32[]{:S(2)}) async-start(bf16[8,40,6144]{2,1,0:T(8,128)(2,1)} %bitcast.107), calls=%async_computation.1 | async-start | bytes 7864320 | tf_op jit(solution)/shard_map/all_to_all | solution.py:42
  108.3 0.2 all-gather.7.cloned.1.call-start
  108.4 0.0 all-gather.9.cloned.1.call-done
  108.5 4.4 %fusion.2 = f32[320,256]{1,0:T(8,128)S(1)} fusion(bf16[320,6144]{1,0:T(8,128)(2,1)} %bitcast.5, bf16[1,256,6144]{2,1,0:T(8,128)(2,1)} %all-gather.9.cloned.1.call-done), kind=kOutput, calls=%fused_computation.7 | convolution fusion | flops 1006632960 | bytes 7405568 | tf_op jit(solution)/shard_map/dot_general | solution.py:21
  112.9 47.6 %all-to-all-done.1 = bf16[8,40,6144]{2,1,0:T(8,128)(2,1)} async-done(((bf16[8,40,6144]{2,1,0:T(8,128)(2,1)}), bf16[8,40,6144]{2,1,0:T(8,128)(2,1)}, u32[]{:S(2)}, u32[]{:S(2)}) %all-to-all-start.1) | async-done | bytes 3932192 | tf_op jit(solution)/shard_map/all_to_all | solution.py:42
  160.5 4.4 %fusion.7 = f32[320,256]{1,0:T(8,128)S(1)} fusion(bf16[320,6144]{1,0:T(8,128)(2,1)} %bitcast.8, bf16[6144,512]{1,0:T(8,128)(2,1)} %all-gather.5.cloned.1.call-done), kind=kOutput, calls=%fused_computation.12 | convolution fusion | flops 1006632960 | bytes 7405568 | tf_op jit(solution)/shard_map/dot_general | solution.py:48
  164.9 0.5 copy-done
  165.4 3.3 multiply_convert_fusion.2
  168.7 0.8 pad_maximum_fusion
  169.6 1.7 fusion.46
  171.2 1.7 fusion.45
  172.9 1.7 fusion.44
  174.6 1.7 fusion.43
  176.2 1.7 fusion.42
  177.9 1.7 fusion.41
  179.6 1.7 fusion.40
  181.2 1.7 fusion.39
  182.9 1.7 fusion.38
  184.6 1.7 fusion.37
  186.3 1.7 fusion.36
  188.0 1.7 fusion.35
  189.6 1.7 fusion.34
  191.4 1.7 fusion.33
  193.1 1.7 fusion.32
  194.7 1.7 fusion.31
  196.4 8.4 %all-to-all-start.3 = ((bf16[16,320,384]{2,1,0:T(8,128)(2,1)}), bf16[16,320,384]{2,1,0:T(8,128)(2,1)}, u32[]{:S(2)}, u32[]{:S(2)}) async-start(bf16[16,320,384]{2,1,0:T(8,128)(2,1)} %fusion.31), calls=%async_computation.3 | async-start | bytes 7864320 | tf_op jit(solution)/shard_map/all_to_all | solution.py:68
  204.8 3.3 fusion.5
  208.2 3.2 fusion
  211.4 63.0 %all-to-all-done.3 = bf16[16,320,384]{2,1,0:T(8,128)(2,1)} async-done(((bf16[16,320,384]{2,1,0:T(8,128)(2,1)}), bf16[16,320,384]{2,1,0:T(8,128)(2,1)}, u32[]{:S(2)}, u32[]{:S(2)}) %all-to-all-start.3) | async-done | bytes 3932192 | tf_op jit(solution)/shard_map/all_to_all | solution.py:68
  274.4 5.2 %all-to-all-start.2 = ((bf16[8,40,6144]{2,1,0:T(8,128)(2,1)}), bf16[8,40,6144]{2,1,0:T(8,128)(2,1)}, u32[]{:S(2)}, u32[]{:S(2)}) async-start(bf16[8,40,6144]{2,1,0:T(8,128)(2,1)} %bitcast.106), calls=%async_computation.2 | async-start | bytes 7864320 | tf_op jit(solution)/shard_map/all_to_all | solution.py:61
  279.6 3.0 copy.25
  282.6 2.8 copy.24
  285.4 51.3 %all-to-all-done.2 = bf16[8,40,6144]{2,1,0:T(8,128)(2,1)} async-done(((bf16[8,40,6144]{2,1,0:T(8,128)(2,1)}), bf16[8,40,6144]{2,1,0:T(8,128)(2,1)}, u32[]{:S(2)}, u32[]{:S(2)}) %all-to-all-start.2) | async-done | bytes 3932192 | tf_op jit(solution)/shard_map/all_to_all | solution.py:61
  336.7 7.3 %all-to-all-start.4 = ((bf16[320,16,384]{2,0,1:T(8,128)(2,1)}), bf16[320,16,384]{2,0,1:T(8,128)(2,1)}, u32[]{:S(2)}, u32[]{:S(2)}) async-start(bf16[320,16,384]{2,0,1:T(8,128)(2,1)} %copy.24), calls=%async_computation.4 | async-start | bytes 7864320 | tf_op jit(solution)/shard_map/all_to_all | solution.py:71
  344.1 9.7 %gather_fusion = bf16[256,6144]{1,0:T(8,128)(2,1)} fusion(bf16[320,6144]{1,0:T(8,128)(2,1)} %bitcast.12, s32[1024]{0:T(1024)S(1)} %pad_clamp_fusion), kind=kCustom, calls=%fused_computation | custom fusion | bytes 6292480 | tf_op jit(solution)/shard_map/gather | solution.py:64
  353.8 6.2 %reshape.96 = bf16[128,2,6144]{2,1,0:T(2,128)(2,1)S(1)} reshape(bf16[256,6144]{1,0:T(8,128)(2,1)} %gather_fusion) | data formatting | bytes 6291456 | tf_op jit(solution)/shard_map/reshape | solution.py:64
  360.0 9.7 %reduce_sum.25 = bf16[128,6144]{1,0:T(8,128)(2,1)} reduce(bf16[128,2,6144]{2,1,0:T(2,128)(2,1)S(1)} %reshape.96, bf16[]{:T(256)} %constant.5.clone.1), dimensions={1}, to_apply=%region_5.6 | reduce | flops 786432 | bytes 4718594 | tf_op jit(solution)/shard_map/reduce_sum | solution.py:65
  369.7 4.9 %fusion.21 = f32[1,384,256]{2,1,0:T(8,128)} fusion(bf16[5120,384]{1,0:T(8,128)(2,1)} %bitcast.29, bf16[5120,768]{1,0:T(8,128)(2,1)} %all-gather.7.cloned.1.call-done), kind=kOutput, calls=%fused_computation.26 | convolution fusion | flops 1006632960 | bytes 6946816 | tf_op jit(solution)/shard_map/dot_general | solution.py:15
  374.6 4.9 %fusion.24 = f32[1,384,256]{2,1,0:T(8,128)} fusion(bf16[5120,384]{1,0:T(8,128)(2,1)} %bitcast.29, bf16[5120,768]{1,0:T(8,128)(2,1)} %all-gather.7.cloned.1.call-done), kind=kOutput, calls=%fused_computation.27 | convolution fusion | flops 1006632960 | bytes 6946816 | tf_op jit(solution)/shard_map/dot_general | solution.py:15
  379.5 19.6 %all-to-all-done.4 = bf16[320,16,384]{2,0,1:T(8,128)(2,1)} async-done(((bf16[320,16,384]{2,0,1:T(8,128)(2,1)}), bf16[320,16,384]{2,0,1:T(8,128)(2,1)}, u32[]{:S(2)}, u32[]{:S(2)}) %all-to-all-start.4) | async-done | bytes 3932192 | tf_op jit(solution)/shard_map/all_to_all | solution.py:71
  399.1 5.2 %fusion.27 = f32[1,256,384]{2,1,0:T(8,128)} fusion(bf16[5120,384]{1,0:T(8,128)(2,1)} %bitcast.33, bf16[5120,768]{1,0:T(8,128)(2,1)} %all-gather.7.cloned.1.call-done), kind=kOutput, calls=%fused_computation.28 | convolution fusion | flops 1006632960 | bytes 6946816 | tf_op jit(solution)/shard_map/dot_general | solution.py:15
  (17 shorter events, 0.1 us)
Async XLA Ops:
  7.2 101.3 %all-gather.9.cloned.1.call-start = ((), (), s32[]{:S(2)}) async-start(), calls=%async_computation.7 | async-start | bytes 3342336 | tf_op jit(solution)/shard_map/all_gather | solution.py:50
  7.9 152.6 %all-gather.5.cloned.1.call-start = ((), (), s32[]{:S(2)}) async-start(), calls=%async_computation.5 | async-start | bytes 6684672 | tf_op jit(solution)/shard_map/all_gather | solution.py:10
  19.5 8.4 %copy-start.1 = (f32[128,2]{0,1:T(2,128)S(1)}, f32[128,2]{0,1:T(2,128)}, u32[]{:S(2)}) copy-start(f32[128,2]{0,1:T(2,128)} %param.10) | copy-start | bytes 3076
  37.7 64.2 %all-to-all-start = ((bf16[8,40,6144]{2,1,0:T(8,128)(2,1)}), bf16[8,40,6144]{2,1,0:T(8,128)(2,1)}, u32[]{:S(2)}, u32[]{:S(2)}) async-start(bf16[8,40,6144]{2,1,0:T(8,128)(2,1)} %bitcast.108), calls=%async_computation | async-start | bytes 7864320 | tf_op jit(solution)/shard_map/all_to_all | solution.py:43
  101.9 58.6 %all-to-all-start.1 = ((bf16[8,40,6144]{2,1,0:T(8,128)(2,1)}), bf16[8,40,6144]{2,1,0:T(8,128)(2,1)}, u32[]{:S(2)}, u32[]{:S(2)}) async-start(bf16[8,40,6144]{2,1,0:T(8,128)(2,1)} %bitcast.107), calls=%async_computation.1 | async-start | bytes 7864320 | tf_op jit(solution)/shard_map/all_to_all | solution.py:42
  108.3 261.5 %all-gather.7.cloned.1.call-start = ((), (), s32[]{:S(2)}) async-start(), calls=%async_computation.6 | async-start | bytes 8355840 | tf_op jit(solution)/shard_map/all_gather | solution.py:10
  160.5 4.9 %copy-start = (bf16[6144,512]{1,0:T(8,128)(2,1)S(1)}, bf16[6144,512]{1,0:T(8,128)(2,1)}, u32[]{:S(2)}) copy-start(bf16[6144,512]{1,0:T(8,128)(2,1)} %all-gather.5.cloned.1.call-done) | copy-start | bytes 18874372
  196.4 11.7 %slice-start = ((s8[6291456]{0:T(1024)(128)(4,1)}), s8[2097152]{0:T(1024)(128)(4,1)S(1)}, s32[]{:S(2)}) async-start(s8[6291456]{0:T(1024)(128)(4,1)} %bitcast.110), calls=%async_computation.8 | async-start | bytes 4194304
  196.4 78.0 %all-to-all-start.3 = ((bf16[16,320,384]{2,1,0:T(8,128)(2,1)}), bf16[16,320,384]{2,1,0:T(8,128)(2,1)}, u32[]{:S(2)}, u32[]{:S(2)}) async-start(bf16[16,320,384]{2,1,0:T(8,128)(2,1)} %fusion.31), calls=%async_computation.3 | async-start | bytes 7864320 | tf_op jit(solution)/shard_map/all_to_all | solution.py:68
  204.8 3.4 slice-start.1
  274.4 62.4 %all-to-all-start.2 = ((bf16[8,40,6144]{2,1,0:T(8,128)(2,1)}), bf16[8,40,6144]{2,1,0:T(8,128)(2,1)}, u32[]{:S(2)}, u32[]{:S(2)}) async-start(bf16[8,40,6144]{2,1,0:T(8,128)(2,1)} %bitcast.106), calls=%async_computation.2 | async-start | bytes 7864320 | tf_op jit(solution)/shard_map/all_to_all | solution.py:61
  336.7 62.3 %all-to-all-start.4 = ((bf16[320,16,384]{2,0,1:T(8,128)(2,1)}), bf16[320,16,384]{2,0,1:T(8,128)(2,1)}, u32[]{:S(2)}, u32[]{:S(2)}) async-start(bf16[320,16,384]{2,0,1:T(8,128)(2,1)} %copy.24), calls=%async_computation.4 | async-start | bytes 7864320 | tf_op jit(solution)/shard_map/all_to_all | solution.py:71
Sparse Core Ops, SparseCore 0:
  9.6 36.6 all-gather.8
  48.6 85.5 all-gather.4
  169.7 82.8 all-gather.6
